TPU v7x, 128 devices: a whole 4x4x4 slice. The times are simulated.
128 devices in a mesh: row: 32 (over y, x, core), col: 4 (over z).
Axes of the slice: x: 4, y: 4, z: 4, core: 2. Of those that a mesh axis runs over, the one named last changes fastest.
Arguments:
- velocity: float32 [512, 512, 2048], P(None, 'row', 'col'), may hold values from -6 to 6
- symbol_x: float32 [512], replicated, may hold values from 0.3 to 3
- symbol_y: float32 [512], replicated, may hold values from 0.3 to 3
- symbol_z: float32 [2048], replicated, may hold values from 0.3 to 3
Outputs:
- coefficients: float32 [512, 512, 2048], P('row', 'col')
All inputs are finite; a program needn't handle non-finite values.
Results may differ from a plain program's by a relative error of at most 0.000076.
Values sent between devices are 32-bit elements; how exact they have to be, the bound alone decides.
A program may use at most 192 MiB of HBM per device.

v0:
```python
import jax
import jax.numpy as jnp
from jax import lax
from jax.sharding import PartitionSpec as P


def cut_along(x, dim, devices):
    dims = x.shape
    parts = x.reshape(*dims[:dim], devices, dims[dim] // devices, *dims[dim + 1 :])
    return jnp.moveaxis(parts, dim, 0)


def cut_rows(length, count):
    lap = length // count
    if lap >= 8:
        lap -= lap % 8
    return [lap * k for k in range(1, count)]


def joined_along(parts, dim):
    parts = jnp.moveaxis(parts, 0, dim)
    dims = parts.shape
    return parts.reshape(*dims[:dim], dims[dim] * dims[dim + 1], *dims[dim + 2 :])


def exchange_in_pieces(x, axis, pieces, split_dim, concat_dim):
    parts = cut_along(x, split_dim, lax.axis_size(axis))
    widest = max(range(1, max(2, parts.ndim - 1)), key=lambda d: parts.shape[d])
    finished = []
    for share in jnp.split(parts, cut_rows(parts.shape[widest], pieces), axis=widest):
        if share.size:
            finished.append(lax.all_to_all(share, axis, split_axis=0, concat_axis=0, tiled=True))
    return joined_along(jnp.concatenate(finished, axis=widest), concat_dim)


def mode_table(count):
    rank = jnp.arange(count)
    angle = 2.0 * jnp.pi / count * (rank[:, None] * rank[None, :] % count).astype(jnp.float32)
    return (jnp.cos(angle) + jnp.sin(angle)) * count ** (-0.5)


def along_dim(values, dim):
    moved = jnp.tensordot(
        values, mode_table(values.shape[dim]), axes=([dim], [0]), precision=lax.Precision.HIGHEST
    )
    return jnp.moveaxis(moved, -1, dim)


def local(velocity, symbol_x, symbol_y, symbol_z):
    part_values = velocity
    part_values = along_dim(part_values, 0)
    part_values = lax.all_to_all(part_values, "row", split_axis=0, concat_axis=1, tiled=True)
    part_values = along_dim(part_values, 1)
    pencil_values = part_values
    pencil_values = exchange_in_pieces(pencil_values, "col", 2, 1, 2)
    pencil_values = along_dim(pencil_values, 2)
    share_x = pencil_values.shape[0]
    part_x = lax.dynamic_slice_in_dim(symbol_x, lax.axis_index("row") * share_x, share_x)
    share_y = pencil_values.shape[1]
    part_y = lax.dynamic_slice_in_dim(symbol_y, lax.axis_index("col") * share_y, share_y)
    symbol = part_x[:, None, None] + part_y[None, :, None] + symbol_z[None, None, :]
    pencil_values = pencil_values * ((1.0 - 0.2 * symbol) / (1.0 + 0.2 * symbol))
    return pencil_values


def solution(mesh):
    placed = (P(None, "row", "col"), P(), P(), P())
    return jax.shard_map(
        local, mesh=mesh, in_specs=placed, out_specs=P("row", "col", None), check_vma=False
    )
```

profile of v0, /device:TPU:1, one launch (start us, length us, event | category | flops | bytes accessed | tf_op | source)
XLA Modules:
  0.0 650.9 jit_solution(2667797766476617710)
XLA Ops:
  0.0 4.2 fusion.53
  4.2 38.0 %fusion.5 = f32[512,16,512]{2,0,1:T(8,128)S(1)} fusion(f32[512,16,512]{2,1,0:T(8,128)} %param.4, f32[512,512,1]{0,1,2:T(8,128)S(1)} %fusion.53), kind=kOutput, calls=%fused_computation.10 | convolution fusion | flops 25769803776 | bytes 34603008 | tf_op jit(solution)/shard_map/dot_general | solution.py:43
  42.2 17.2 %copy.9 = f32[512,16,512]{2,1,0:T(8,128)S(1)} copy(f32[512,16,512]{2,0,1:T(8,128)S(1)} %fusion.5) | data formatting | bytes 33554432 | tf_op jit(solution)/shard_map/dot_general | solution.py:43
  59.5 194.0 %all_to_all.28 = f32[512,16,512]{2,1,0:T(8,128)S(1)} all-to-all(f32[512,16,512]{2,1,0:T(8,128)S(1)} %copy.9), channel_id=1, replica_groups=mesh['row'=32,'col'=4] {'row'}, dimensions={0} | all-to-all | bytes 33554432 | tf_op jit(solution)/shard_map/all_to_all | solution.py:52
  253.4 6.4 copy.10
  259.8 44.5 %fusion.25 = f32[16,512,512]{1,2,0:T(8,128)} fusion(f32[16,512,512]{2,1,0:T(8,128)} %bitcast.37), kind=kOutput, calls=%fused_computation.31 | convolution fusion | flops 25773998080 | bytes 33554432 | tf_op jit(solution)/shard_map/dot_general | solution.py:43
  304.3 7.0 %copy.18 = f32[16,4,128,512]{3,2,0,1:T(8,128)S(1)} copy(f32[16,4,128,512]{3,2,1,0:T(8,128)} %bitcast.38) | data formatting | bytes 33554432 | tf_op jit(solution)/shard_map/reshape | solution.py:9
  311.3 6.9 %fusion.46 = (f32[4,16,64,512]{3,2,1,0:T(8,128)}, f32[4,16,64,512]{3,2,1,0:T(8,128)}) fusion(f32[4,16,128,512]{3,2,1,0:T(8,128)S(1)} %bitcast.35), kind=kLoop, calls=%fused_computation.54 | loop fusion | bytes 33554432 | tf_op jit(solution)/shard_map/split | solution.py:30
  318.2 101.9 %all_to_all.29 = f32[4,16,64,512]{3,2,1,0:T(8,128)} all-to-all(f32[4,16,64,512]{3,2,1,0:T(8,128)} %get-tuple-element.5), channel_id=1, replica_groups=mesh['row'=32,'col'=4] {'col'}, dimensions={0} | all-to-all | bytes 16777216 | tf_op jit(solution)/shard_map/all_to_all | solution.py:32
  420.1 5.6 all-to-all-start.2
  425.8 0.8 dynamic_slice.7
  426.5 0.8 dynamic_slice.6
  427.3 0.1 broadcast_add_fusion
  427.3 67.7 %fusion.4.clone.4 = f32[2048,2048,1]{1,0,2:T(8,128)} fusion(), kind=kLoop, calls=%fused_computation.8.clone.clone.clone.1 | loop fusion | flops 67108864 | bytes 16777216 | tf_op jit(solution)/shard_map/mul | solution.py:62
  495.0 23.5 %all-to-all-done.2 = f32[4,16,64,512]{3,2,1,0:T(8,128)} async-done(((f32[4,16,64,512]{3,2,1,0:T(8,128)}), f32[4,16,64,512]{3,2,1,0:T(8,128)}, u32[]{:S(2)}, u32[]{:S(2)}) %all-to-all-start.2) | async-done | bytes 8388640 | tf_op jit(solution)/shard_map/all_to_all | solution.py:32
  518.6 6.9 %maximum_bitcast_fusion = f32[4,16,16,8,512]{4,3,2,1,0:T(8,128)S(1)} fusion(f32[4,16,64,512]{3,2,1,0:T(8,128)} %all-to-all-done.2, f32[4,16,64,512]{3,2,1,0:T(8,128)} %all_to_all.29), kind=kLoop, calls=%fused_computation.6 | loop fusion | flops 4194304 | bytes 33554432
  525.5 0.0 copy-start
  525.5 6.2 copy.13
  531.7 0.0 copy-done
  531.7 119.0 %divide_multiply_fusion = f32[16,128,2048]{2,1,0:T(8,128)} fusion(f32[2048]{0:T(1024)S(1)} %copy-done, f32[16,128]{1,0:T(8,128)S(1)} %broadcast_add_fusion, f32[16,128,2048]{2,1,0:T(8,128)} %bitcast.39, f32[2048,2048,1]{1,0,2:T(8,128)} %fusion.4.clone.4), kind=kOutput, calls=%fused_computation.12 | convolution fusion | flops 103104380928 | bytes 50348032 | tf_op jit(solution)/shard_map/dot_general | solution.py:43
Async XLA Ops:
  420.1 98.5 %all-to-all-start.2 = ((f32[4,16,64,512]{3,2,1,0:T(8,128)}), f32[4,16,64,512]{3,2,1,0:T(8,128)}, u32[]{:S(2)}, u32[]{:S(2)}) async-start(f32[4,16,64,512]{3,2,1,0:T(8,128)} %get-tuple-element.6), calls=%async_computation.2 | async-start | bytes 16777216 | tf_op jit(solution)/shard_map/all_to_all | solution.py:32
  525.5 6.2 copy-start
where the time goes:
time: 662 us; the launch traced here: 651 us
  blocking collectives  296 us (45%)
  matrix products  202 us (31%)
  other arithmetic  78.8 us (12%)
  local copies, waits for them, and re-layouts  45.2 us (7%)
  waiting for transfers between devices  23.5 us (4%)
    dot_general x3, matrix products, along_dim(): jnp.tensordot(values, mode_table(values.shape[dim]), axes=([dim], [0]), p...  202 us
    all_to_all x1, blocking collectives, local(): lax.all_to_all(part_values, 'row', split_axis=0, concat_axis=1, tiled=True)  194 us
    all_to_all x1, blocking collectives, exchange_in_pieces(): lax.all_to_all(share, axis, split_axis=0, concat_axis=0, tiled=True)  102 us
    mul x1, other arithmetic, local(): pencil_values * ((1.0 - 0.2 * symbol) / (1.0 + 0.2 * symbol))  67.7 us
    all_to_all x1, waiting for transfers between devices, exchange_in_pieces(): lax.all_to_all(share, axis, split_axis=0, concat_axis=0, tiled=True)  23.5 us
    dot_general x1, local copies, waits for them, and re-layouts, along_dim(): jnp.tensordot(values, mode_table(values.shape[dim]), axes=([dim], [0]), p...  17.2 us
  transfers between devices with their start and end apart: 1, of which 1 were waited for; matrix products, arithmetic and copies ran while one was open for 11% of the time, Pallas kernels for 0%

commit v1 on v0

v1 whole, which is shorter than its diff:
```python
import functools

import jax
import jax.numpy as jnp
import numpy as np
from jax import lax
from jax.experimental import pallas as pl
from jax.experimental.pallas import tpu as pltpu
from jax.sharding import PartitionSpec as P

MESH = pl.DeviceIdType.MESH
F32 = jnp.float32
BF16 = jnp.bfloat16
FINE = 32


def split(values):
    head = values.astype(BF16)
    return head, (values - head.astype(F32)).astype(BF16)


def mode_table(count):
    rank = np.arange(count)
    angle = 2.0 * np.pi / count * (rank[:, None] * rank[None, :] % count)
    return ((np.cos(angle) + np.sin(angle)) / np.sqrt(count)).astype(np.float32)


def stacked_table(count):
    table = mode_table(count)
    head = table.astype(BF16)
    rest = (table - head.astype(np.float32)).astype(BF16)
    return np.concatenate([head, rest, head], axis=1)


def factor_tables(count):
    k = np.arange(count)
    coarse = 2.0 * np.pi / count * (FINE * np.arange(count // FINE)[:, None] * k % count)
    fine = 2.0 * np.pi / count * (np.arange(FINE)[:, None] * k % count)
    scale = 1.0 / np.sqrt(count)
    tables = np.cos(coarse), np.sin(coarse), (np.cos(fine) + np.sin(fine)) * scale, (np.cos(fine) - np.sin(fine)) * scale
    return [t.astype(np.float32) for t in tables]


def x_kernel(v_ref, h_ref, o_ref, parts):
    nx, ny, lanes = v_ref.shape
    v = v_ref.reshape(nx * ny, lanes)
    o = o_ref.reshape(nx * ny, lanes)
    for y in range(ny):
        head, rest = split(v[pl.ds(y, nx, stride=ny), :])
        at = pl.ds(y * lanes, lanes)
        parts[0:nx, at] = head
        parts[nx : 2 * nx, at] = head
        parts[2 * nx : 3 * nx, at] = rest
    for y in range(0, ny, 2):
        made = jnp.dot(h_ref[...], parts[:, y * lanes : (y + 2) * lanes], preferred_element_type=F32)
        o[pl.ds(y, nx, stride=ny), :] = made[:, :lanes]
        o[pl.ds(y + 1, nx, stride=ny), :] = made[:, lanes:]


def x_transform(velocity, table):
    nx, ny, nz = velocity.shape
    block = pl.BlockSpec((nx, 8, 128), lambda y, z: (0, y, z))
    return pl.pallas_call(
        x_kernel,
        grid=(ny // 8, nz // 128),
        in_specs=[block, pl.BlockSpec(table.shape, lambda y, z: (0, 0))],
        out_specs=block,
        out_shape=jax.ShapeDtypeStruct(velocity.shape, F32),
        scratch_shapes=[pltpu.VMEM((3 * nx, 8 * 128), BF16)],
        compiler_params=pltpu.CompilerParams(vmem_limit_bytes=40 * 2**20),
    )(velocity, table)


def exchange_kernel(
    rows, cols, sent, h_ref, cos_ref, sin_ref, plus_ref, minus_ref, out,
    got_y, got_z, t_head, t_rest, made_y, made_z, parts_y, parts_z,
    row_send, row_recv, own_sem, col_send, col_recv, out_sem,
):
    chunks, ny, zs = got_y.shape
    ys, nz = got_z.shape[1:]
    yl = ny // rows
    row, col = lax.axis_index("row"), lax.axis_index("col")

    barrier = pltpu.get_barrier_semaphore()

    @pl.loop(1, rows)
    def _(o):
        pl.semaphore_signal(barrier, inc=1, device_id={"row": lax.rem(row + o, rows)}, device_id_type=MESH)

    for d in range(1, cols):
        pl.semaphore_signal(barrier, inc=1, device_id={"col": lax.rem(col + d, cols)}, device_id_type=MESH)
    pl.semaphore_wait(barrier, rows + cols - 2)

    mine = pl.ds(pl.multiple_of(row * yl, yl), yl)

    @pl.loop(0, chunks)
    def _(j):
        @pl.loop(1, rows)
        def _(o):
            y = lax.rem(row // 8 + o // 8, 4)
            x = lax.rem(row // 2 + o // 2, 4)
            c = lax.rem(row + o, 2)
            p = y * 8 + x * 2 + c
            pltpu.make_async_remote_copy(
                src_ref=sent.at[p * chunks + j], dst_ref=got_y.at[j, mine],
                send_sem=row_send, recv_sem=row_recv.at[j], device_id={"row": p}, device_id_type=MESH,
            ).start()

        pltpu.make_async_copy(sent.at[row * chunks + j], got_y.at[j, mine], own_sem.at[j]).start()

    @pl.loop(0, nz // FINE)
    def _(i):
        table = cos_ref[pl.ds(i, 1), :] * plus_ref[...] + sin_ref[pl.ds(i, 1), :] * minus_ref[...]
        head, rest = split(table)
        at = pl.ds(pl.multiple_of(i * FINE, FINE), FINE)
        t_head[at, :] = head
        t_rest[at, :] = rest

    def col_sends(j, slot):
        return [
            pltpu.make_async_remote_copy(
                src_ref=made_y.at[slot, pl.ds(pl.multiple_of(q * ys, ys), ys)],
                dst_ref=got_z.at[j, :, pl.ds(pl.multiple_of(col * zs, zs), zs)],
                send_sem=col_send.at[slot], recv_sem=col_recv.at[j], device_id={"col": q}, device_id_type=MESH,
            )
            for q in [lax.rem(col + d, cols) for d in (1, 3, 2)]
        ]

    def wait_sends(slot):
        sends = made_y.at[slot, pl.ds(0, (cols - 1) * ys)]
        pltpu.make_async_copy(sends, sends, col_send.at[slot]).wait()

    def wait_out(j, slot):
        pltpu.make_async_copy(made_z.at[slot], out.at[j], out_sem.at[slot]).wait()

    def y_step(j):
        slot = lax.rem(j, 2)
        pltpu.make_async_copy(sent.at[row * chunks + j], got_y.at[j, mine], own_sem.at[j]).wait()
        landed = got_y.at[j, pl.ds(0, (rows - 1) * yl)]
        pltpu.make_async_copy(landed, landed, row_recv.at[j]).wait()
        head, rest = split(got_y[j])
        parts_y[0:ny, :] = head
        parts_y[ny : 2 * ny, :] = head
        parts_y[2 * ny : 3 * ny, :] = rest

        @pl.when(j >= 2)
        def _():
            wait_sends(slot)

        @pl.loop(0, zs // 256)
        def _(n):
            at = pl.ds(pl.multiple_of(n * 256, 256), 256)
            made_y[slot, :, at] = jnp.dot(h_ref[...], parts_y[:, at], preferred_element_type=F32)

        got_z[j, :, pl.ds(pl.multiple_of(col * zs, zs), zs)] = made_y[slot, pl.ds(pl.multiple_of(col * ys, ys), ys), :]
        for copy in col_sends(j, slot):
            copy.start()

    def z_step(j):
        slot = lax.rem(j, 2)
        landed = got_z.at[j, :, pl.ds(0, (cols - 1) * zs)]
        pltpu.make_async_copy(landed, landed, col_recv.at[j]).wait()
        head, rest = split(got_z[j])
        parts_z[0:ys, :] = head
        parts_z[ys : 2 * ys, :] = rest

        @pl.when(j >= 2)
        def _():
            wait_out(j - 2, slot)

        @pl.loop(0, nz // 512)
        def _(n):
            at = pl.ds(pl.multiple_of(n * 512, 512), 512)
            both = jnp.dot(parts_z[...], t_head[:, at], preferred_element_type=F32)
            small = jnp.dot(parts_z[0:ys, :], t_rest[:, at], preferred_element_type=F32)
            made_z[slot, :, at] = both[:ys] + (both[ys:] + small)

        pltpu.make_async_copy(made_z.at[slot], out.at[j], out_sem.at[slot]).start()

    @pl.loop(0, chunks + 1)
    def _(t):
        @pl.when(t < chunks)
        def _():
            y_step(t)

        @pl.when(t >= 1)
        def _():
            z_step(t - 1)

    for slot in range(2):
        wait_sends(slot)
        wait_out(chunks - 2 + slot, slot)
    gone = sent.at[pl.ds(0, (rows - 1) * chunks)]
    pltpu.make_async_copy(gone, gone, row_send).wait()


def exchange(sent, table, factors, rows, cols):
    nx, yl, zs = sent.shape
    chunks, ny, nz = nx // rows, yl * rows, zs * cols
    ys = ny // cols
    anywhere = pl.BlockSpec(memory_space=pl.ANY)
    vmem = pl.BlockSpec(memory_space=pltpu.VMEM)
    dma = pltpu.SemaphoreType.DMA
    return pl.pallas_call(
        functools.partial(exchange_kernel, rows, cols),
        in_specs=[anywhere] + [vmem] * 5,
        out_specs=anywhere,
        out_shape=jax.ShapeDtypeStruct((chunks, ys, nz), F32),
        scratch_shapes=[
            pltpu.VMEM((chunks, ny, zs), F32),
            pltpu.VMEM((chunks, ys, nz), F32),
            pltpu.VMEM((nz, nz), BF16),
            pltpu.VMEM((nz, nz), BF16),
            pltpu.VMEM((2, ny, zs), F32),
            pltpu.VMEM((2, ys, nz), F32),
            pltpu.VMEM((3 * ny, zs), BF16),
            pltpu.VMEM((2 * ys, nz), BF16),
            dma, dma((chunks,)), dma((chunks,)), dma((2,)), dma((chunks,)), dma((2,)),
        ],
        compiler_params=pltpu.CompilerParams(collective_id=0, has_side_effects=True, vmem_limit_bytes=67043328),
    )(sent, table, *factors)


def solution(mesh):
    rows, cols = mesh.shape["row"], mesh.shape["col"]

    def local(velocity, symbol_x, symbol_y, symbol_z):
        table = jnp.asarray(stacked_table(velocity.shape[0]))
        factors = [jnp.asarray(t) for t in factor_tables(velocity.shape[2] * cols)]
        values = x_transform(velocity, table)
        values = exchange(values, table, factors, rows, cols)
        share_x, share_y = values.shape[:2]
        part_x = lax.dynamic_slice_in_dim(symbol_x, lax.axis_index("row") * share_x, share_x)
        part_y = lax.dynamic_slice_in_dim(symbol_y, lax.axis_index("col") * share_y, share_y)
        symbol = part_x[:, None, None] + part_y[None, :, None] + symbol_z[None, None, :]
        return values * ((1.0 - 0.2 * symbol) / (1.0 + 0.2 * symbol))

    placed = (P(None, "row", "col"), P(), P(), P())
    return jax.shard_map(local, mesh=mesh, in_specs=placed, out_specs=P("row", "col", None), check_vma=False)
```

time: 662 us -> 258 us (0.39); the launches traced: 651 us -> 258 us
  blocking collectives: 296 us -> 0 us
  Pallas kernels: 0 us -> 242 us
  matrix products: 202 us -> 0 us
  other arithmetic: 78.8 us -> 12.9 us
  local copies, waits for them, and re-layouts: 45.2 us -> 2.92 us
  waiting for transfers between devices: 23.5 us -> 0 us
    all_to_all x2 -> x0, blocking collectives: 296 us -> none  [the longest x1 194 us: local(): lax.all_to_all(part_values, 'row', split_axis=0, concat_axis=1, tiled=True)]
    pallas_call x0 -> x2, Pallas kernels: none -> 242 us  [the longest x1 220 us: exchange(): pl.pallas_call(functools.partial(exchange_kernel, rows, cols), in_specs=[...]
    dot_general x3 -> x0, matrix products: 202 us -> none  [along_dim(): jnp.tensordot(values, mode_table(values.shape[dim]), axes=([dim], [0]), p...]
    mul x1, other arithmetic: 67.7 us -> 12.8 us  [local(): return values * ((1.0 - 0.2 * symbol) / (1.0 + 0.2 * symbol))]
    all_to_all x1 -> x0, waiting for transfers between devices: 23.5 us -> none  [exchange_in_pieces(): lax.all_to_all(share, axis, split_axis=0, concat_axis=0, tiled=True)]
    dot_general x1 -> x0, local copies, waits for them, and re-layouts: 17.2 us -> none  [along_dim(): jnp.tensordot(values, mode_table(values.shape[dim]), axes=([dim], [0]), p...]
    reshape x2 -> x0, local copies, waits for them, and re-layouts: 13.2 us -> none  [the longest x1 6.95 us: cut_along(): x.reshape(*dims[:dim], devices, dims[dim] // devices, *dims[dim + 1:])]
    split x1 -> x0, local copies, waits for them, and re-layouts: 6.94 us -> none  [exchange_in_pieces(): jnp.split(parts, cut_rows(parts.shape[widest], pieces), axis=widest)]
  transfers between devices with their start and end apart: 1 -> 0, of which waited for: 1 -> 0; matrix products, arithmetic and copies ran while one was open for 11% -> 0% of each run, Pallas kernels for 0% -> 0%
where the time goes in v1:
time: 258 us
  Pallas kernels  242 us (94%)
  other arithmetic  12.9 us (5%)
  local copies, waits for them, and re-layouts  2.92 us (1%)
    pallas_call x1, Pallas kernels, exchange(): pl.pallas_call(functools.partial(exchange_kernel, rows, cols), in_specs=[...  220 us
    pallas_call x1, Pallas kernels, x_transform(): pl.pallas_call(x_kernel, grid=(ny // 8, nz // 128), in_specs=[block, pl.B...  21.7 us
    mul x1, other arithmetic, local(): return values * ((1.0 - 0.2 * symbol) / (1.0 + 0.2 * symbol))  12.8 us

profile of v1, /device:TPU:1, one launch (start us, length us, event | category | flops | bytes accessed | tf_op | source)
XLA Modules:
  0.0 257.6 jit_solution(3464645070210379079)
XLA Ops:
  0.0 0.0 copy-start
  0.0 1.4 copy-done
  1.4 21.7 %shard_map.91.sent = f32[512,16,512]{2,1,0:T(8,128)} custom-call(f32[512,16,512]{2,1,0:T(8,128)} %v_ref.1, bf16[512,1536]{1,0:T(8,128)(2,1)S(1)} %copy-done), custom_call_target="tpu_custom_call" | custom-call | tf_op jit(solution)/shard_map/pallas_call | solution.py:63
  23.1 220.0 %shard_map.92 = f32[16,128,2048]{2,1,0:T(8,128)} custom-call(f32[512,16,512]{2,1,0:T(8,128)} %shard_map.91.sent, bf16[512,1536]{1,0:T(8,128)(2,1)} %constant.31.clone.h_ref, f32[64,2048]{1,0:T(8,128)} %constant.32.clone.cos_ref, f32[64,2048]{1,0:T(8,128)} %constant.33.clone.sin_ref, f32[32,2048]{1,0:T(8,128)} %constant.34.clone.plus_ref, ...), custom_call_target="tpu_custom_call" | custom-call | tf_op jit(solution)/shard_map/pallas_call | solution.py:204
  243.2 0.8 dynamic_slice.7
  243.9 0.8 dynamic_slice.6
  244.7 0.1 broadcast_add_fusion
  244.8 12.8 %divide_multiply_fusion = f32[16,128,2048]{2,1,0:T(8,128)} fusion(f32[16,128,2048]{2,1,0:T(8,128)} %shard_map.92, f32[2048]{0:T(1024)} %param.12, f32[16,128]{1,0:T(8,128)S(1)} %broadcast_add_fusion), kind=kLoop, calls=%fused_computation | loop fusion | flops 25165824 | bytes 33570816 | tf_op jit(solution)/shard_map/mul | solution.py:236
Async XLA Ops:
  0.0 1.4 copy-start

commit v2 on v0

v2 whole, which is shorter than its diff:
```python
import functools

import jax
import jax.numpy as jnp
import numpy as np
from jax import lax
from jax.experimental import pallas as pl
from jax.experimental.pallas import tpu as pltpu
from jax.sharding import PartitionSpec as P

MESH = pl.DeviceIdType.MESH
F32 = jnp.float32
BF16 = jnp.bfloat16
FINE = 32
LANES = 128
Y_BLOCK = 8
AHEAD = 4
Y_LAG = 3
SLOTS = 4


def split(values):
    head = values.astype(BF16)
    return head, (values - head.astype(F32)).astype(BF16)


def mode_table(count):
    rank = np.arange(count)
    angle = 2.0 * np.pi / count * (rank[:, None] * rank[None, :] % count)
    return ((np.cos(angle) + np.sin(angle)) / np.sqrt(count)).astype(np.float32)


def stacked_table(count):
    table = mode_table(count)
    head = table.astype(BF16)
    rest = (table - head.astype(np.float32)).astype(BF16)
    return np.concatenate([head, rest, head], axis=1)


def factor_tables(count):
    k = np.arange(count)
    coarse = 2.0 * np.pi / count * (FINE * np.arange(count // 2 // FINE)[:, None] * k % count)
    fine = 2.0 * np.pi / count * (np.arange(FINE)[:, None] * k % count)
    scale = 1.0 / np.sqrt(count)
    tables = np.cos(coarse), np.sin(coarse), (np.cos(fine) + np.sin(fine)) * scale, (np.cos(fine) - np.sin(fine)) * scale
    return [t.astype(np.float32) for t in tables]


def kernel(
    rows, cols, velocity, h_ref, cos_ref, sin_ref, plus_ref, minus_ref, sx_ref, sy_ref, sz_ref, out, sent,
    v_in, v_out, parts_x, got_y, got_z, t_head, t_rest, made_y, made_z, parts_y, parts_z, sy_col,
    in_sem, keep_sem, row_send, row_recv, own_sem, col_send, col_recv, out_sem,
):
    nx, yl, zs = velocity.shape
    chunks, ys, nz = out.shape
    ny = yl * rows
    quarters = zs // LANES
    units = chunks * quarters
    halves = yl // Y_BLOCK
    blocks = quarters * halves
    early = blocks
    row, col = lax.axis_index("row"), lax.axis_index("col")
    mine = pl.ds(pl.multiple_of(row * yl, yl), yl)

    def place(u):
        first = lax.div(units + early - 1 - u, units)
        j = first * lax.rem(u, 2) + (1 - first) * lax.div(u, quarters)
        q = first * lax.div(u, 2) + (1 - first) * lax.rem(u, quarters)
        return j, q

    def block_of(ref, b):
        y, z = lax.rem(b, halves), lax.div(b, halves)
        return ref.at[:, pl.ds(pl.multiple_of(y * Y_BLOCK, Y_BLOCK), Y_BLOCK), pl.ds(pl.multiple_of(z * LANES, LANES), LANES)]

    def kept_at(b):
        y, z = lax.rem(b, halves), lax.div(b, halves)
        return sent.at[z, :, pl.ds(pl.multiple_of(y * Y_BLOCK, Y_BLOCK), Y_BLOCK), :]

    def load(b):
        slot = lax.rem(b, 2)
        return pltpu.make_async_copy(block_of(velocity, b), v_in.at[slot], in_sem.at[slot])

    def keep(b):
        slot = lax.rem(b, 2)
        return pltpu.make_async_copy(v_out.at[slot], kept_at(b), keep_sem.at[slot])

    def x_step(b):
        slot = lax.rem(b, 2)
        load(b).wait()
        v = v_in.at[slot].reshape(nx * Y_BLOCK, LANES)
        o = v_out.at[slot].reshape(nx * Y_BLOCK, LANES)
        for y in range(0, Y_BLOCK, 2):
            for n in (y, y + 1):
                head, rest = split(v[pl.ds(n, nx, stride=Y_BLOCK), :])
                at = pl.ds(n * LANES, LANES)
                parts_x[0:nx, at] = head
                parts_x[nx : 2 * nx, at] = head
                parts_x[2 * nx : 3 * nx, at] = rest
            made = jnp.dot(h_ref[...], parts_x[:, y * LANES : (y + 2) * LANES], preferred_element_type=F32)
            o[pl.ds(y, nx, stride=Y_BLOCK), :] = made[:, :LANES]
            o[pl.ds(y + 1, nx, stride=Y_BLOCK), :] = made[:, LANES:]
        keep(b).start()

        @pl.when(b + 2 < blocks)
        def _():
            load(b + 2).start()

    def own(u):
        j, q = place(u)
        return pltpu.make_async_copy(sent.at[q, row * chunks + j], got_y.at[u, mine], own_sem.at[u])

    def row_sends(u):
        j, q = place(u)

        @pl.loop(1, rows)
        def _(o):
            y = lax.rem(lax.div(row, 8) + lax.div(o, 8), 4)
            x = lax.rem(lax.div(row, 2) + lax.div(o, 2), 4)
            c = lax.rem(row + o, 2)
            p = y * 8 + x * 2 + c
            pltpu.make_async_remote_copy(
                src_ref=sent.at[q, p * chunks + j], dst_ref=got_y.at[u, mine],
                send_sem=row_send, recv_sem=row_recv.at[u], device_id={"row": p}, device_id_type=MESH,
            ).start()

        own(u).start()

    def wait_sends(slot):
        sends = made_y.at[slot, pl.ds(0, (cols - 1) * ys)]
        pltpu.make_async_copy(sends, sends, col_send.at[slot]).wait()

    def y_step(u):
        slot = lax.rem(u, SLOTS)
        j, q = place(u)
        own(u).wait()
        landed = got_y.at[u, pl.ds(0, (rows - 1) * yl)]
        pltpu.make_async_copy(landed, landed, row_recv.at[u]).wait()
        head, rest = split(got_y[u])
        parts_y[0:ny, :] = head
        parts_y[ny : 2 * ny, :] = head
        parts_y[2 * ny : 3 * ny, :] = rest

        @pl.when(u >= SLOTS)
        def _():
            wait_sends(slot)

        made_y[slot] = jnp.dot(h_ref[...], parts_y[...], preferred_element_type=F32)
        to = got_z.at[j, col * quarters + q]
        to[...] = made_y[slot, pl.ds(pl.multiple_of(col * ys, ys), ys), :]
        for d in (1, 3, 2):
            p = lax.rem(col + d, cols)
            pltpu.make_async_remote_copy(
                src_ref=made_y.at[slot, pl.ds(pl.multiple_of(p * ys, ys), ys)], dst_ref=to,
                send_sem=col_send.at[slot], recv_sem=col_recv.at[j], device_id={"col": p}, device_id_type=MESH,
            ).start()

    def wait_out(j, slot):
        pltpu.make_async_copy(made_z.at[slot], out.at[j], out_sem.at[slot]).wait()

    def z_step(j):
        slot = lax.rem(j, 2)
        landed = got_z.at[j, pl.ds(0, (cols - 1) * quarters)]
        pltpu.make_async_copy(landed, landed, col_recv.at[j]).wait()
        fold = cols * quarters // 2
        for k in range(fold):
            low, high = got_z[j, k], got_z[j, k + fold]
            at = pl.ds(k * LANES, LANES)
            for n, value in enumerate((low + high, low - high)):
                head, rest = split(value)
                parts_z[n * ys : (n + 1) * ys, at] = head
                parts_z[(n + 2) * ys : (n + 3) * ys, at] = rest

        @pl.when(j >= 2)
        def _():
            wait_out(j - 2, slot)

        part = sx_ref[row * chunks + j] + sy_col[...]
        even = lax.rem(lax.broadcasted_iota(jnp.int32, (ys, LANES), 1), 2) == 0

        @pl.loop(0, nz // 512)
        def _(n):
            at = pl.ds(pl.multiple_of(n * 512, 512), 512)
            both = jnp.dot(parts_z[...], t_head[:, at], preferred_element_type=F32)
            small = jnp.dot(parts_z[0 : 2 * ys, :], t_rest[:, at], preferred_element_type=F32)
            total = both[: 2 * ys] + (both[2 * ys :] + small)
            for m in range(512 // LANES):
                lanes = slice(m * LANES, (m + 1) * LANES)
                value = jnp.where(even, total[:ys, lanes], total[ys:, lanes])
                to = pl.ds(pl.multiple_of(n * 512 + m * LANES, LANES), LANES)
                symbol = part + sz_ref[:, to]
                made_z[slot, :, to] = value * ((1.0 - 0.2 * symbol) / (1.0 + 0.2 * symbol))

        pltpu.make_async_copy(made_z.at[slot], out.at[j], out_sem.at[slot]).start()

    load(0).start()
    load(1).start()
    barrier = pltpu.get_barrier_semaphore()

    @pl.loop(1, rows)
    def _(o):
        pl.semaphore_signal(barrier, inc=1, device_id={"row": lax.rem(row + o, rows)}, device_id_type=MESH)

    for d in range(1, cols):
        pl.semaphore_signal(barrier, inc=1, device_id={"col": lax.rem(col + d, cols)}, device_id_type=MESH)

    @pl.loop(0, halves)
    def _(t):
        x_step(t)

    pl.semaphore_wait(barrier, rows + cols - 2)

    @pl.loop(halves - 1, 4 * chunks + 9)
    def _(t):
        @pl.when(jnp.logical_and(t >= halves, t < blocks))
        def _():
            x_step(t)

        @pl.when(t < blocks)
        def _():
            @pl.when(lax.rem(t, halves) == halves - 1)
            def _():
                for h in range(halves):
                    keep(t - (halves - 1) + h).wait()

                @pl.loop(t - 1, t + 1)
                def _(u):
                    row_sends(u)

        @pl.when(t == blocks)
        def _():
            @pl.loop(0, nz // 2 // FINE)
            def _(i):
                table = cos_ref[pl.ds(i, 1), :] * plus_ref[...] + sin_ref[pl.ds(i, 1), :] * minus_ref[...]
                head, rest = split(table)
                at = pl.ds(pl.multiple_of(i * FINE, FINE), FINE)
                t_head[at, :] = head
                t_rest[at, :] = rest

            spread = jnp.broadcast_to(sy_ref[:, pl.ds(pl.multiple_of(col * ys, ys), ys)], (LANES, ys))
            sy_col[...] = spread.T

        @pl.when(jnp.logical_and(t >= blocks - 1, t < units - AHEAD))
        def _():
            late = lax.div(units + blocks - 1 - t, units)

            @pl.loop(t + AHEAD - late * (AHEAD - 1), t + AHEAD + 1)
            def _(u):
                row_sends(u)

        @pl.when(jnp.logical_and(t >= Y_LAG, t < units + Y_LAG))
        def _():
            y_step(t - Y_LAG)

        @pl.when(jnp.logical_and(t >= 12, lax.rem(t, 4) == 0))
        def _():
            z_step(lax.div(t, 4) - 3)

    for slot in range(SLOTS):
        wait_sends(slot)
    for slot in range(2):
        wait_out(chunks - 2 + slot, slot)
    gone = sent.at[:, pl.ds(0, (rows - 1) * chunks)]
    pltpu.make_async_copy(gone, gone, row_send).wait()


def solution(mesh):
    rows, cols = mesh.shape["row"], mesh.shape["col"]

    def local(velocity, symbol_x, symbol_y, symbol_z):
        nx, yl, zs = velocity.shape
        chunks, ny, nz = nx // rows, yl * rows, zs * cols
        ys, quarters = ny // cols, zs // LANES
        units = chunks * quarters
        table = jnp.asarray(stacked_table(nx))
        factors = [jnp.asarray(t) for t in factor_tables(nz)]
        anywhere = pl.BlockSpec(memory_space=pl.ANY)
        vmem = pl.BlockSpec(memory_space=pltpu.VMEM)
        dma = pltpu.SemaphoreType.DMA
        out, _ = pl.pallas_call(
            functools.partial(kernel, rows, cols),
            in_specs=[anywhere] + [vmem] * 5 + [pl.BlockSpec(memory_space=pltpu.SMEM), vmem, vmem],
            out_specs=(anywhere, anywhere),
            out_shape=(
                jax.ShapeDtypeStruct((chunks, ys, nz), F32),
                jax.ShapeDtypeStruct((quarters, nx, yl, LANES), F32),
            ),
            scratch_shapes=[
                pltpu.VMEM((2, nx, Y_BLOCK, LANES), F32),
                pltpu.VMEM((2, nx, Y_BLOCK, LANES), F32),
                pltpu.VMEM((3 * nx, Y_BLOCK * LANES), BF16),
                pltpu.VMEM((units, ny, LANES), F32),
                pltpu.VMEM((chunks, nz // LANES, ys, LANES), F32),
                pltpu.VMEM((nz // 2, nz), BF16),
                pltpu.VMEM((nz // 2, nz), BF16),
                pltpu.VMEM((SLOTS, ny, LANES), F32),
                pltpu.VMEM((2, ys, nz), F32),
                pltpu.VMEM((3 * ny, LANES), BF16),
                pltpu.VMEM((4 * ys, nz // 2), BF16),
                pltpu.VMEM((ys, LANES), F32),
                dma((2,)), dma((2,)), dma, dma((units,)), dma((units,)), dma((SLOTS,)), dma((chunks,)), dma((2,)),
            ],
            compiler_params=pltpu.CompilerParams(collective_id=0, has_side_effects=True, vmem_limit_bytes=67043328),
        )(velocity, table, *factors, symbol_x, symbol_y[None, :], symbol_z[None, :])
        return out

    placed = (P(None, "row", "col"), P(), P(), P())
    return jax.shard_map(local, mesh=mesh, in_specs=placed, out_specs=P("row", "col", None), check_vma=False)
```

time: 662 us -> 234 us (0.35); the launches traced: 651 us -> 233 us
  blocking collectives: 296 us -> 0 us
  Pallas kernels: 0 us -> 221 us
  matrix products: 202 us -> 0 us
  other arithmetic: 78.8 us -> 0 us
  local copies, waits for them, and re-layouts: 45.2 us -> 11.8 us
  waiting for transfers between devices: 23.5 us -> 0 us
    all_to_all x2 -> x0, blocking collectives: 296 us -> none  [the longest x1 194 us: local(): lax.all_to_all(part_values, 'row', split_axis=0, concat_axis=1, tiled=True)]
    pallas_call x0 -> x1, Pallas kernels: none -> 221 us  [local(): pl.pallas_call(functools.partial(kernel, rows, cols), in_specs=[anywhere]...]
    dot_general x3 -> x0, matrix products: 202 us -> none  [along_dim(): jnp.tensordot(values, mode_table(values.shape[dim]), axes=([dim], [0]), p...]
    mul x1 -> x0, other arithmetic: 67.7 us -> none  [local(): pencil_values * ((1.0 - 0.2 * symbol) / (1.0 + 0.2 * symbol))]
    all_to_all x1 -> x0, waiting for transfers between devices: 23.5 us -> none  [exchange_in_pieces(): lax.all_to_all(share, axis, split_axis=0, concat_axis=0, tiled=True)]
    dot_general x1 -> x0, local copies, waits for them, and re-layouts: 17.2 us -> none  [along_dim(): jnp.tensordot(values, mode_table(values.shape[dim]), axes=([dim], [0]), p...]
    reshape x2 -> x0, local copies, waits for them, and re-layouts: 13.2 us -> none  [the longest x1 6.95 us: cut_along(): x.reshape(*dims[:dim], devices, dims[dim] // devices, *dims[dim + 1:])]
    unnamed x2 -> x1, local copies, waits for them, and re-layouts: 0.01 us -> 11.8 us
  transfers between devices with their start and end apart: 1 -> 0, of which waited for: 1 -> 0; matrix products, arithmetic and copies ran while one was open for 11% -> 0% of each run, Pallas kernels for 0% -> 0%
where the time goes in v2:
time: 234 us; the launch traced here: 233 us
  Pallas kernels  221 us (94%)
  local copies, waits for them, and re-layouts  11.8 us (5%)
    pallas_call x1, Pallas kernels, local(): pl.pallas_call(functools.partial(kernel, rows, cols), in_specs=[anywhere]...  221 us
    unnamed x1, local copies, waits for them, and re-layouts  11.8 us

profile of v2, /device:TPU:1, one launch (start us, length us, event | category | flops | bytes accessed | tf_op | source)
XLA Modules:
  0.0 233.2 jit_solution(9102686202047171018)
XLA Ops:
  0.0 221.4 %shard_map.91 = (f32[16,128,2048]{2,1,0:T(8,128)}, f32[4,512,16,128]{3,2,1,0:T(8,128)}) custom-call(f32[512,16,512]{2,1,0:T(8,128)} %velocity.1, bf16[512,1536]{1,0:T(8,128)(2,1)} %constant.10.clone.h_ref, f32[32,2048]{1,0:T(8,128)} %constant.11.clone.cos_ref, f32[32,2048]{1,0:T(8,128)} %constant.12.clone.sin_ref, f32[32,2048]{1,0:T(8,128)} %constant.13.clone.plus_ref, ...), custom_call_target="tpu_custom_call" | custom-call | tf_op jit(solution)/shard_map/pallas_call | solution.py:279
  221.4 11.8 %copy.11 = f32[16,128,2048]{2,1,0:T(8,128)} copy(f32[16,128,2048]{2,1,0:T(8,128)} %get-tuple-element.6) | data formatting | bytes 33554432

commit v3 on v2

--- a/solution.py
+++ b/solution.py
@@ -48,8 +48,8 @@
 
 def kernel(
     rows, cols, velocity, h_ref, cos_ref, sin_ref, plus_ref, minus_ref, sx_ref, sy_ref, sz_ref, out, sent,
-    v_in, v_out, parts_x, got_y, got_z, t_head, t_rest, made_y, made_z, parts_y, parts_z, sy_col,
-    in_sem, keep_sem, row_send, row_recv, own_sem, col_send, col_recv, out_sem,
+    got_y, got_z, t_head, t_rest, made_y, parts_y, parts_z, sy_col,
+    in_sem, keep_sem, row_send, row_recv, own_sem, col_send, col_recv, free_sem,
 ):
     nx, yl, zs = velocity.shape
     chunks, ys, nz = out.shape
@@ -62,6 +62,11 @@
     row, col = lax.axis_index("row"), lax.axis_index("col")
     mine = pl.ds(pl.multiple_of(row * yl, yl), yl)
 
+    ring_y = [lax.rem(lax.div(row, 8) + d, 4) * 8 for d in range(4)]
+    ring_x = [lax.rem(lax.div(row, 2) + d, 4) * 2 for d in range(4)]
+    pair = [lax.rem(row + d, 2) for d in range(2)]
+    peers = [ring_y[o // 8] + ring_x[o // 2 % 4] + pair[o % 2] for o in range(1, rows)]
+
     def place(u):
         first = lax.div(units + early - 1 - u, units)
         j = first * lax.rem(u, 2) + (1 - first) * lax.div(u, quarters)
@@ -76,27 +81,36 @@
         y, z = lax.rem(b, halves), lax.div(b, halves)
         return sent.at[z, :, pl.ds(pl.multiple_of(y * Y_BLOCK, Y_BLOCK), Y_BLOCK), :]
 
+    late = chunks // 2
+    tiles = got_z.reshape(chunks * nz * ys // LANES // Y_BLOCK, Y_BLOCK, LANES)
+    lines = got_z.reshape(chunks * nz * ys // LANES, LANES)
+    base = late * nz * ys // LANES // Y_BLOCK
+
     def load(b):
         slot = lax.rem(b, 2)
-        return pltpu.make_async_copy(block_of(velocity, b), v_in.at[slot], in_sem.at[slot])
+        at = pl.ds(base + slot * nx, nx)
+        return pltpu.make_async_copy(block_of(velocity, b), tiles.at[at], in_sem.at[slot])
 
     def keep(b):
         slot = lax.rem(b, 2)
-        return pltpu.make_async_copy(v_out.at[slot], kept_at(b), keep_sem.at[slot])
+        at = pl.ds(base + (2 + slot) * nx, nx)
+        return pltpu.make_async_copy(tiles.at[at], kept_at(b), keep_sem.at[slot])
 
     def x_step(b):
         slot = lax.rem(b, 2)
         load(b).wait()
-        v = v_in.at[slot].reshape(nx * Y_BLOCK, LANES)
-        o = v_out.at[slot].reshape(nx * Y_BLOCK, LANES)
+        v = lines.at[pl.ds(pl.multiple_of((base + slot * nx) * Y_BLOCK, Y_BLOCK), nx * Y_BLOCK)]
+        o = lines.at[pl.ds(pl.multiple_of((base + (2 + slot) * nx) * Y_BLOCK, Y_BLOCK), nx * Y_BLOCK)]
         for y in range(0, Y_BLOCK, 2):
             for n in (y, y + 1):
                 head, rest = split(v[pl.ds(n, nx, stride=Y_BLOCK), :])
                 at = pl.ds(n * LANES, LANES)
-                parts_x[0:nx, at] = head
-                parts_x[nx : 2 * nx, at] = head
-                parts_x[2 * nx : 3 * nx, at] = rest
-            made = jnp.dot(h_ref[...], parts_x[:, y * LANES : (y + 2) * LANES], preferred_element_type=F32)
+                t_head[0:nx, at] = head
+                t_head[nx : 2 * nx, at] = head
+                t_rest[0:nx, at] = rest
+            lanes = slice(y * LANES, (y + 2) * LANES)
+            made = jnp.dot(h_ref[:, : 2 * nx], t_head[0 : 2 * nx, lanes], preferred_element_type=F32)
+            made += jnp.dot(h_ref[:, 2 * nx :], t_rest[0:nx, lanes], preferred_element_type=F32)
             o[pl.ds(y, nx, stride=Y_BLOCK), :] = made[:, :LANES]
             o[pl.ds(y + 1, nx, stride=Y_BLOCK), :] = made[:, LANES:]
         keep(b).start()
@@ -112,14 +126,10 @@
     def row_sends(u):
         j, q = place(u)
 
-        @pl.loop(1, rows)
-        def _(o):
-            y = lax.rem(lax.div(row, 8) + lax.div(o, 8), 4)
-            x = lax.rem(lax.div(row, 2) + lax.div(o, 2), 4)
-            c = lax.rem(row + o, 2)
-            p = y * 8 + x * 2 + c
+        to = got_y.at[u, mine]
+        for p in peers:
             pltpu.make_async_remote_copy(
-                src_ref=sent.at[q, p * chunks + j], dst_ref=got_y.at[u, mine],
+                src_ref=sent.at[q, p * chunks + j], dst_ref=to,
                 send_sem=row_send, recv_sem=row_recv.at[u], device_id={"row": p}, device_id_type=MESH,
             ).start()
 
@@ -144,6 +154,10 @@
         def _():
             wait_sends(slot)
 
+        @pl.when(u == late * quarters)
+        def _():
+            pl.semaphore_wait(free_sem, cols - 1)
+
         made_y[slot] = jnp.dot(h_ref[...], parts_y[...], preferred_element_type=F32)
         to = got_z.at[j, col * quarters + q]
         to[...] = made_y[slot, pl.ds(pl.multiple_of(col * ys, ys), ys), :]
@@ -154,11 +168,7 @@
                 send_sem=col_send.at[slot], recv_sem=col_recv.at[j], device_id={"col": p}, device_id_type=MESH,
             ).start()
 
-    def wait_out(j, slot):
-        pltpu.make_async_copy(made_z.at[slot], out.at[j], out_sem.at[slot]).wait()
-
     def z_step(j):
-        slot = lax.rem(j, 2)
         landed = got_z.at[j, pl.ds(0, (cols - 1) * quarters)]
         pltpu.make_async_copy(landed, landed, col_recv.at[j]).wait()
         fold = cols * quarters // 2
@@ -169,10 +179,6 @@
                 head, rest = split(value)
                 parts_z[n * ys : (n + 1) * ys, at] = head
                 parts_z[(n + 2) * ys : (n + 3) * ys, at] = rest
-
-        @pl.when(j >= 2)
-        def _():
-            wait_out(j - 2, slot)
 
         part = sx_ref[row * chunks + j] + sy_col[...]
         even = lax.rem(lax.broadcasted_iota(jnp.int32, (ys, LANES), 1), 2) == 0
@@ -188,9 +194,7 @@
                 value = jnp.where(even, total[:ys, lanes], total[ys:, lanes])
                 to = pl.ds(pl.multiple_of(n * 512 + m * LANES, LANES), LANES)
                 symbol = part + sz_ref[:, to]
-                made_z[slot, :, to] = value * ((1.0 - 0.2 * symbol) / (1.0 + 0.2 * symbol))
-
-        pltpu.make_async_copy(made_z.at[slot], out.at[j], out_sem.at[slot]).start()
+                out[j, :, to] = value * ((1.0 - 0.2 * symbol) / (1.0 + 0.2 * symbol))
 
     load(0).start()
     load(1).start()
@@ -225,6 +229,12 @@
                 @pl.loop(t - 1, t + 1)
                 def _(u):
                     row_sends(u)
+
+                @pl.when(t == blocks - 1)
+                def _():
+                    for d in range(1, cols):
+                        p = lax.rem(col + d, cols)
+                        pl.semaphore_signal(free_sem, inc=1, device_id={"col": p}, device_id_type=MESH)
 
         @pl.when(t == blocks)
         def _():
@@ -241,9 +251,9 @@
 
         @pl.when(jnp.logical_and(t >= blocks - 1, t < units - AHEAD))
         def _():
-            late = lax.div(units + blocks - 1 - t, units)
-
-            @pl.loop(t + AHEAD - late * (AHEAD - 1), t + AHEAD + 1)
+            last = lax.div(units + blocks - 1 - t, units)
+
+            @pl.loop(t + AHEAD - last * (AHEAD - 1), t + AHEAD + 1)
             def _(u):
                 row_sends(u)
 
@@ -257,8 +267,6 @@
 
     for slot in range(SLOTS):
         wait_sends(slot)
-    for slot in range(2):
-        wait_out(chunks - 2 + slot, slot)
     gone = sent.at[:, pl.ds(0, (rows - 1) * chunks)]
     pltpu.make_async_copy(gone, gone, row_send).wait()
 
@@ -279,27 +287,24 @@
         out, _ = pl.pallas_call(
             functools.partial(kernel, rows, cols),
             in_specs=[anywhere] + [vmem] * 5 + [pl.BlockSpec(memory_space=pltpu.SMEM), vmem, vmem],
-            out_specs=(anywhere, anywhere),
+            out_specs=(vmem, anywhere),
             out_shape=(
-                jax.ShapeDtypeStruct((chunks, ys, nz), F32),
+                pltpu.VMEM((chunks, ys, nz), F32),
                 jax.ShapeDtypeStruct((quarters, nx, yl, LANES), F32),
             ),
             scratch_shapes=[
-                pltpu.VMEM((2, nx, Y_BLOCK, LANES), F32),
-                pltpu.VMEM((2, nx, Y_BLOCK, LANES), F32),
-                pltpu.VMEM((3 * nx, Y_BLOCK * LANES), BF16),
                 pltpu.VMEM((units, ny, LANES), F32),
                 pltpu.VMEM((chunks, nz // LANES, ys, LANES), F32),
                 pltpu.VMEM((nz // 2, nz), BF16),
                 pltpu.VMEM((nz // 2, nz), BF16),
                 pltpu.VMEM((SLOTS, ny, LANES), F32),
-                pltpu.VMEM((2, ys, nz), F32),
                 pltpu.VMEM((3 * ny, LANES), BF16),
                 pltpu.VMEM((4 * ys, nz // 2), BF16),
                 pltpu.VMEM((ys, LANES), F32),
-                dma((2,)), dma((2,)), dma, dma((units,)), dma((units,)), dma((SLOTS,)), dma((chunks,)), dma((2,)),
+                dma((2,)), dma((2,)), dma, dma((units,)), dma((units,)), dma((SLOTS,)), dma((chunks,)),
+                pltpu.SemaphoreType.REGULAR,
             ],
-            compiler_params=pltpu.CompilerParams(collective_id=0, has_side_effects=True, vmem_limit_bytes=67043328),
+            compiler_params=pltpu.CompilerParams(collective_id=0, has_side_effects=True, vmem_limit_bytes=46 * 2**20),
         )(velocity, table, *factors, symbol_x, symbol_y[None, :], symbol_z[None, :])
         return out
 

time: 234 us -> 224 us (0.957)
  local copies, waits for them, and re-layouts: 11.8 us -> 6.16 us
  Pallas kernels: 221 us -> 218 us
    unnamed x1, local copies, waits for them, and re-layouts: 11.8 us -> 6.16 us
    pallas_call x1, Pallas kernels: 221 us -> 218 us  [local(): pl.pallas_call(functools.partial(kernel, rows, cols), in_specs=[anywhere]...]
where the time goes in v3:
time: 224 us
  Pallas kernels  218 us (97%)
  local copies, waits for them, and re-layouts  6.16 us (3%)
    pallas_call x1, Pallas kernels, local(): pl.pallas_call(functools.partial(kernel, rows, cols), in_specs=[anywhere]...  218 us
    unnamed x1, local copies, waits for them, and re-layouts  6.16 us

profile of v3, /device:TPU:1, one launch (start us, length us, event | category | flops | bytes accessed | tf_op | source)
XLA Modules:
  0.0 224.1 jit_solution(5045396874282783642)
XLA Ops:
  0.0 217.9 %shard_map.91 = (f32[16,128,2048]{2,1,0:T(8,128)S(1)}, f32[4,512,16,128]{3,2,1,0:T(8,128)}) custom-call(f32[512,16,512]{2,1,0:T(8,128)} %velocity.1, bf16[512,1536]{1,0:T(8,128)(2,1)} %constant.10.clone.h_ref, f32[32,2048]{1,0:T(8,128)} %constant.11.clone.cos_ref, f32[32,2048]{1,0:T(8,128)} %constant.12.clone.sin_ref, f32[32,2048]{1,0:T(8,128)} %constant.13.clone.plus_ref, ...), custom_call_target="tpu_custom_call" | custom-call | tf_op jit(solution)/shard_map/pallas_call | solution.py:287
  217.9 6.2 %copy.11 = f32[16,128,2048]{2,1,0:T(8,128)} copy(f32[16,128,2048]{2,1,0:T(8,128)S(1)} %get-tuple-element.6) | data formatting | bytes 33554432

commit v4 on v3

--- a/solution.py
+++ b/solution.py
@@ -14,9 +14,10 @@
 FINE = 32
 LANES = 128
 Y_BLOCK = 8
+FIRST = 4
 AHEAD = 4
 Y_LAG = 3
-SLOTS = 4
+SLOTS = 8
 
 
 def split(values):
@@ -58,19 +59,20 @@
     units = chunks * quarters
     halves = yl // Y_BLOCK
     blocks = quarters * halves
-    early = blocks
+    early = FIRST * quarters
     row, col = lax.axis_index("row"), lax.axis_index("col")
     mine = pl.ds(pl.multiple_of(row * yl, yl), yl)
 
     ring_y = [lax.rem(lax.div(row, 8) + d, 4) * 8 for d in range(4)]
     ring_x = [lax.rem(lax.div(row, 2) + d, 4) * 2 for d in range(4)]
     pair = [lax.rem(row + d, 2) for d in range(2)]
-    peers = [ring_y[o // 8] + ring_x[o // 2 % 4] + pair[o % 2] for o in range(1, rows)]
+    far = sorted(range(1, rows), key=lambda o: -(min(o // 8, 4 - o // 8) + min(o // 2 % 4, 4 - o // 2 % 4)))
+    peers = [ring_y[o // 8] + ring_x[o // 2 % 4] + pair[o % 2] for o in far]
 
     def place(u):
         first = lax.div(units + early - 1 - u, units)
-        j = first * lax.rem(u, 2) + (1 - first) * lax.div(u, quarters)
-        q = first * lax.div(u, 2) + (1 - first) * lax.rem(u, quarters)
+        j = first * lax.rem(u, FIRST) + (1 - first) * lax.div(u, quarters)
+        q = first * lax.div(u, FIRST) + (1 - first) * lax.rem(u, quarters)
         return j, q
 
     def block_of(ref, b):
@@ -226,7 +228,9 @@
                 for h in range(halves):
                     keep(t - (halves - 1) + h).wait()
 
-                @pl.loop(t - 1, t + 1)
+                ready = lax.div(t, halves) * FIRST
+
+                @pl.loop(ready, ready + FIRST)
                 def _(u):
                     row_sends(u)
 
@@ -236,9 +240,20 @@
                         p = lax.rem(col + d, cols)
                         pl.semaphore_signal(free_sem, inc=1, device_id={"col": p}, device_id_type=MESH)
 
-        @pl.when(t == blocks)
-        def _():
-            @pl.loop(0, nz // 2 // FINE)
+        @pl.when(jnp.logical_and(t >= early - AHEAD, t < units - AHEAD))
+        def _():
+            row_sends(t + AHEAD)
+
+        @pl.when(jnp.logical_and(t >= Y_LAG, t < units + Y_LAG))
+        def _():
+            y_step(t - Y_LAG)
+
+        @pl.when(jnp.logical_and(t >= blocks + 1, t < blocks + 9))
+        def _():
+            share = nz // 2 // FINE // 8
+            start = (t - blocks - 1) * share
+
+            @pl.loop(start, start + share)
             def _(i):
                 table = cos_ref[pl.ds(i, 1), :] * plus_ref[...] + sin_ref[pl.ds(i, 1), :] * minus_ref[...]
                 head, rest = split(table)
@@ -249,21 +264,12 @@
             spread = jnp.broadcast_to(sy_ref[:, pl.ds(pl.multiple_of(col * ys, ys), ys)], (LANES, ys))
             sy_col[...] = spread.T
 
-        @pl.when(jnp.logical_and(t >= blocks - 1, t < units - AHEAD))
-        def _():
-            last = lax.div(units + blocks - 1 - t, units)
-
-            @pl.loop(t + AHEAD - last * (AHEAD - 1), t + AHEAD + 1)
-            def _(u):
-                row_sends(u)
-
-        @pl.when(jnp.logical_and(t >= Y_LAG, t < units + Y_LAG))
-        def _():
-            y_step(t - Y_LAG)
-
-        @pl.when(jnp.logical_and(t >= 12, lax.rem(t, 4) == 0))
-        def _():
-            z_step(lax.div(t, 4) - 3)
+        first = lax.div(128 + 25 - t, 128)
+        often = jnp.logical_and(jnp.logical_and(t >= 18, t < 26), lax.rem(t, 2) == 0)
+
+        @pl.when(jnp.logical_or(often, jnp.logical_and(t >= 28, lax.rem(t, 4) == 0)))
+        def _():
+            z_step(first * (lax.div(t, 2) - 9) + (1 - first) * (lax.div(t, 4) - 3))
 
     for slot in range(SLOTS):
         wait_sends(slot)
@@ -304,7 +310,7 @@
                 dma((2,)), dma((2,)), dma, dma((units,)), dma((units,)), dma((SLOTS,)), dma((chunks,)),
                 pltpu.SemaphoreType.REGULAR,
             ],
-            compiler_params=pltpu.CompilerParams(collective_id=0, has_side_effects=True, vmem_limit_bytes=46 * 2**20),
+            compiler_params=pltpu.CompilerParams(collective_id=0, has_side_effects=True, vmem_limit_bytes=47 * 2**20),
         )(velocity, table, *factors, symbol_x, symbol_y[None, :], symbol_z[None, :])
         return out
 

time: 224 us -> 222 us (level); the launches traced: 224 us -> 219 us
  Pallas kernels: 218 us -> 213 us
    pallas_call x1, Pallas kernels: 218 us -> 213 us  [local(): pl.pallas_call(functools.partial(kernel, rows, cols), in_specs=[anywhere]...]
where the time goes in v4:
time: 222 us; the launch traced here: 219 us
  Pallas kernels  213 us (96%)
  local copies, waits for them, and re-layouts  6.16 us (3%)
    pallas_call x1, Pallas kernels, local(): pl.pallas_call(functools.partial(kernel, rows, cols), in_specs=[anywhere]...  213 us
    unnamed x1, local copies, waits for them, and re-layouts  6.16 us

profile of v4, /device:TPU:1, one launch (start us, length us, event | category | flops | bytes accessed | tf_op | source)
XLA Modules:
  0.0 219.5 jit_solution(5506000647972250775)
XLA Ops:
  0.0 213.3 %shard_map.91 = (f32[16,128,2048]{2,1,0:T(8,128)S(1)}, f32[4,512,16,128]{3,2,1,0:T(8,128)}) custom-call(f32[512,16,512]{2,1,0:T(8,128)} %velocity.1, bf16[512,1536]{1,0:T(8,128)(2,1)} %constant.10.clone.h_ref, f32[32,2048]{1,0:T(8,128)} %constant.11.clone.cos_ref, f32[32,2048]{1,0:T(8,128)} %constant.12.clone.sin_ref, f32[32,2048]{1,0:T(8,128)} %constant.13.clone.plus_ref, ...), custom_call_target="tpu_custom_call" | custom-call | tf_op jit(solution)/shard_map/pallas_call | solution.py:293
  213.3 6.2 %copy.11 = f32[16,128,2048]{2,1,0:T(8,128)} copy(f32[16,128,2048]{2,1,0:T(8,128)S(1)} %get-tuple-element.6) | data formatting | bytes 33554432
